TPU v7x, 32 devices: a whole 2x2x4 slice. The times are simulated.
32 devices in a mesh: up: 8 (over z, core), down: 4 (over y, x).
Axes of the slice: x: 2, y: 2, z: 4, core: 2. Of those that a mesh axis runs over, the one named last changes fastest.
Arguments:
- deltas: bfloat16 [256, 4096], P('down', 'up'), may hold values from -6 to 6
- gradients: bfloat16 [256, 4096], P('up', 'down'), may hold values from -0.375 to 0.375
- up_blocks: int32 [8, 16], P(None, 'up'), may hold values from 0 to 3, as said below
- down_blocks: int32 [16], P('down'), may hold values from 0 to 7, as said below
- decoder: bfloat16 [4096, 4608], P('up', 'down'), may hold values from -0.09375 to 0.09375
- encoder: bfloat16 [4608, 4096], P('up', 'down'), may hold values from -6 to 6
Outputs:
- edge_scores: float32 [4096, 4096], P('up', 'down')
Inputs may be any that keep to these rules, and one draw needn't show every extreme that they name: `up_blocks`: for each window and each index i of up, the 2 entries in columns i * 2 to (i + 1) * 2 - 1 are distinct. `down_blocks`: for each index j of down, the 4 entries j * 4 to (j + 1) * 4 - 1 are distinct.
All inputs are finite; a program needn't handle non-finite values.
Results may differ from a plain program's by a relative error of at most 0.0003.
Values may be sent and summed in bfloat16 or wider, within the bound.
A program may use at most 64 MiB of HBM per device.

v0:
```python
import jax
import jax.numpy as jnp
from jax import lax
from jax.sharding import PartitionSpec as P

UF_DEV = 512
VF_DEV = 1024
BLOCK = 128
DACT = 4
WIN = 32


def local(deltas, gradients, up_blocks, down_blocks, decoder, encoder):
    token_deltas = lax.all_gather(deltas, "down", axis=0, tiled=True)
    token_grads = lax.all_gather(gradients, "up", axis=0, tiled=True)
    tokens_all = token_deltas.shape[0]
    windows = tokens_all // WIN
    row_blocks = UF_DEV // BLOCK
    col_blocks = VF_DEV // BLOCK
    local_ids = jnp.arange(row_blocks, dtype=jnp.int32)
    block_on = jnp.any(up_blocks[:, :, None] == local_ids[None, None, :], axis=1)
    masked = token_deltas.reshape(windows, WIN, row_blocks, BLOCK) * block_on[
        :, None, :, None
    ].astype(token_deltas.dtype)
    masked = masked.reshape(tokens_all, UF_DEV)
    dec_whole = lax.all_gather(decoder, "down", axis=1, tiled=True)
    enc_height = encoder.shape[0]
    enc_used = jnp.take(
        encoder.reshape(enc_height, col_blocks, BLOCK), down_blocks, axis=1
    ).reshape(enc_height, DACT * BLOCK)
    virtual = jnp.dot(
        dec_whole,
        lax.all_gather(enc_used, "up", axis=0, tiled=True),
        preferred_element_type=jnp.float32,
    )
    grad_used = jnp.take(
        token_grads.reshape(tokens_all, col_blocks, BLOCK), down_blocks, axis=1
    ).reshape(tokens_all, DACT * BLOCK)
    product = lax.dot_general(
        masked, grad_used, (((0,), (0,)), ((), ())), preferred_element_type=jnp.float32
    )
    scored = (product * virtual).reshape(UF_DEV, DACT, BLOCK)
    filled = jnp.zeros((UF_DEV, col_blocks, BLOCK), jnp.float32).at[:, down_blocks, :].set(scored)
    return filled.reshape(UF_DEV, VF_DEV)


def solution(mesh):
    placed = (
        P("down", "up"),
        P("up", "down"),
        P(None, "up"),
        P("down"),
        P("up", "down"),
        P("up", "down"),
    )
    return jax.shard_map(
        local, mesh=mesh, in_specs=placed, out_specs=P("up", "down"), check_vma=False
    )
```

profile of v0, /device:TPU:0, one launch (start us, length us, event | category | flops | bytes accessed | tf_op | source)
XLA Modules:
  0.0 144.0 jit_solution(9845222064683501501)
XLA Ops:
  6.5 0.0 copy-start
  6.5 0.0 copy-start.4
  6.5 0.0 all-gather.5.cloned.1.call-start
  6.5 0.7 all-gather.5.cloned.1.call-update
  7.3 0.0 all-gather.3.cloned.1.call-start
  7.3 0.7 compare_select_fusion
  8.0 0.0 copy-done
  8.0 0.0 copy-start.1
  8.0 0.2 copy_bitcast_fusion
  8.2 0.7 gather_fusion.1
  8.9 0.0 copy-done.4
  8.9 0.1 broadcast_bitcast_fusion
  9.0 0.9 bitcast_select_fusion
  9.9 0.0 copy-start.3
  9.9 0.0 copy-start.2
  9.9 0.0 all-gather.3.cloned.1.call-update
  9.9 0.0 copy-done.1
  9.9 16.5 %all_gather.13 = bf16[256,1024]{1,0:T(8,128)(2,1)S(1)} all-gather(bf16[32,1024]{1,0:T(8,128)(2,1)S(1)} %copy-done.1), channel_id=1, replica_groups=mesh['up'=8,'down'=4] {'up'}, dimensions={0}, use_global_device_ids=true | all-gather | bytes 589824 | tf_op jit(solution)/shard_map/all_gather | solution.py:15
  26.4 0.2 copy.32
  26.6 0.3 copy.33
  26.9 0.6 gather_fusion
  27.5 0.1 copy.34
  27.7 0.0 copy-done.3
  27.7 0.1 copy.31
  27.8 0.0 copy-done.2
  27.8 10.0 %all_gather.12 = bf16[256,512]{1,0:T(8,128)(2,1)S(1)} all-gather(bf16[64,512]{1,0:T(8,128)(2,1)S(1)} %copy-done.2), channel_id=1, replica_groups=mesh['up'=8,'down'=4] {'down'}, dimensions={0}, use_global_device_ids=true | all-gather | bytes 327680 | tf_op jit(solution)/shard_map/all_gather | solution.py:14
  37.8 0.1 bitcast_select_fusion.1
  38.0 0.1 mul.14
  38.1 0.3 fusion.1
  38.4 31.6 %all-gather.5.cloned.1.call-done = bf16[512,4608]{1,0:T(8,128)(2,1)} async-done(((bf16[512,1152]{1,0:T(8,128)(2,1)}), bf16[512,4608]{1,0:T(8,128)(2,1)}) %all-gather.5.cloned.1.call-update) | async-done | bytes 4718608 | tf_op jit(solution)/shard_map/all_gather | solution.py:26
  70.1 52.9 %all-gather.3.cloned.1.call-done = bf16[4608,512]{1,0:T(8,128)(2,1)} async-done(((bf16[576,512]{1,0:T(8,128)(2,1)}), bf16[4608,512]{1,0:T(8,128)(2,1)}) %all-gather.3.cloned.1.call-update) | async-done | bytes 4718608 | tf_op jit(solution)/shard_map/all_gather | solution.py:33
  122.9 6.1 %fusion = f32[512,512]{0,1:T(8,128)S(1)} fusion(f32[512,512]{0,1:T(8,128)S(1)} %fusion.1, bf16[4608,512]{1,0:T(8,128)(2,1)} %all-gather.3.cloned.1.call-done, bf16[512,4608]{1,0:T(8,128)(2,1)} %all-gather.5.cloned.1.call-done), kind=kOutput, calls=%fused_computation.4 | convolution fusion | flops 2416181248 | bytes 11534336 | tf_op jit(solution)/shard_map/dot_general | solution.py:31
  129.1 1.3 copy.37
  130.4 0.1 broadcast_in_dim.33
  130.5 1.9 %scatter_fusion = f32[512,8,128]{2,0,1:T(8,128)S(1)} fusion(f32[512,8,128]{2,0,1:T(8,128)S(1)} %broadcast_in_dim.33, s32[4]{0:T(128)S(1)} %compare_select_fusion, f32[4,512,128]{2,1,0:T(8,128)} %bitcast.33), kind=kCustom, calls=%fused_computation.2 | custom fusion | bytes 3145744 | tf_op jit(solution)/shard_map/scatter | solution.py:43
  132.4 1.9 %copy.38 = f32[512,8,128]{0,2,1:T(8,128)} copy(f32[512,8,128]{2,0,1:T(8,128)S(1)} %scatter_fusion) | data formatting | bytes 4194304 | tf_op jit(solution)/shard_map/scatter | solution.py:43
  134.3 2.9 %copy.39 = f32[512,1024]{1,0:T(8,128)} copy(f32[512,1024]{0,1:T(8,128)} %bitcast.32) | data formatting | bytes 4194304 | tf_op jit(solution)/shard_map/reshape | solution.py:44
  (4 shorter events, 0.0 us)
Async XLA Ops:
  6.5 1.4 %copy-start = (bf16[576,1024]{1,0:T(8,128)(2,1)S(1)}, bf16[576,1024]{1,0:T(8,128)(2,1)}, u32[]{:S(2)}) copy-start(bf16[576,1024]{1,0:T(8,128)(2,1)} %param.11) | copy-start | bytes 3538948
  6.5 2.3 %copy-start.4 = (s32[4]{0:T(128)S(1)}, s32[4]{0:T(128)}, u32[]{:S(2)}) copy-start(s32[4]{0:T(128)} %param.9) | copy-start | bytes 52
  6.5 63.5 %all-gather.5.cloned.1.call-start = ((), (), s32[]{:S(2)}) async-start(), calls=%async_computation.1 | async-start | bytes 5898240 | tf_op jit(solution)/shard_map/all_gather | solution.py:26
  7.3 115.7 %all-gather.3.cloned.1.call-start = ((), (), s32[]{:S(2)}) async-start(), calls=%async_computation | async-start | bytes 5308416 | tf_op jit(solution)/shard_map/all_gather | solution.py:33
  8.0 2.0 %copy-start.1 = (bf16[32,1024]{1,0:T(8,128)(2,1)S(1)}, bf16[32,1024]{1,0:T(8,128)(2,1)}, u32[]{:S(2)}) copy-start(bf16[32,1024]{1,0:T(8,128)(2,1)} %param.7) | copy-start | bytes 196612
  9.9 17.8 %copy-start.3 = (s32[8,2]{0,1:T(2,128)S(1)}, s32[8,2]{0,1:T(2,128)}, u32[]{:S(2)}) copy-start(s32[8,2]{0,1:T(2,128)} %param.8) | copy-start | bytes 196
  9.9 17.9 %copy-start.2 = (bf16[64,512]{1,0:T(8,128)(2,1)S(1)}, bf16[64,512]{1,0:T(8,128)(2,1)}, u32[]{:S(2)}) copy-start(bf16[64,512]{1,0:T(8,128)(2,1)} %param.6) | copy-start | bytes 196612
Sparse Core Ops, SparseCore 0:
  9.2 60.8 all-gather.4
  71.7 51.1 all-gather.2
where the time goes:
time: 144 us
  waiting for transfers between devices  85.2 us (59%)
  blocking collectives  26.5 us (18%)
  between operations  13.5 us (9%)
  local copies, waits for them, and re-layouts  10.6 us (7%)
  matrix products  6.41 us (4%)
  other arithmetic  1.76 us (1%)
    all_gather x1, waiting for transfers between devices, local(): lax.all_gather(enc_used, 'up', axis=0, tiled=True)  52.9 us
    all_gather x1, waiting for transfers between devices, local(): dec_whole = lax.all_gather(decoder, 'down', axis=1, tiled=True)  31.6 us
    all_gather x1, blocking collectives, local(): token_grads = lax.all_gather(gradients, 'up', axis=0, tiled=True)  16.5 us
    all_gather x1, blocking collectives, local(): token_deltas = lax.all_gather(deltas, 'down', axis=0, tiled=True)  10 us
    dot_general x1, matrix products, local(): jnp.dot(dec_whole, lax.all_gather(enc_used, 'up', axis=0, tiled=True), pr...  6.1 us
    scatter x2, local copies, waits for them, and re-layouts, local(): jnp.zeros((UF_DEV, col_blocks, BLOCK), jnp.float32).at[:, down_blocks, :]  3.82 us
  transfers between devices with their start and end apart: 2, of which 2 were waited for; matrix products, arithmetic and copies ran while one was open for 3% of the time, Pallas kernels for 0%

commit v1 on v0

--- a/solution.py
+++ b/solution.py
@@ -23,7 +23,7 @@
         :, None, :, None
     ].astype(token_deltas.dtype)
     masked = masked.reshape(tokens_all, UF_DEV)
-    dec_whole = lax.all_gather(decoder, "down", axis=1, tiled=True)
+    dec_whole = jnp.concatenate(lax.all_gather(decoder, "down"), axis=1)
     enc_height = encoder.shape[0]
     enc_used = jnp.take(
         encoder.reshape(enc_height, col_blocks, BLOCK), down_blocks, axis=1

time: 144 us -> 144 us (level)
  waiting for transfers between devices: 85.2 us -> 78.6 us
  local copies, waits for them, and re-layouts: 10.6 us -> 17.2 us
    all_gather x1, waiting for transfers between devices: 52.9 us -> 46.2 us  [local(): lax.all_gather(enc_used, 'up', axis=0, tiled=True)]
    reshape x0 -> x1, local copies, waits for them, and re-layouts: none -> 6.64 us  [local(): dec_whole = jnp.concatenate(lax.all_gather(decoder, 'down'), axis=1)]
  transfers between devices with their start and end apart: 2 -> 2, of which waited for: 2 -> 2; matrix products, arithmetic and copies ran while one was open for 3% -> 8% of each run, Pallas kernels for 0% -> 0%
where the time goes in v1:
time: 144 us
  waiting for transfers between devices  78.6 us (55%)
  blocking collectives  26.5 us (18%)
  local copies, waits for them, and re-layouts  17.2 us (12%)
  between operations  13.5 us (9%)
  matrix products  6.38 us (4%)
  other arithmetic  1.75 us (1%)
    all_gather x1, waiting for transfers between devices, local(): lax.all_gather(enc_used, 'up', axis=0, tiled=True)  46.2 us
    all_gather x1, waiting for transfers between devices, local(): dec_whole = jnp.concatenate(lax.all_gather(decoder, 'down'), axis=1)  31.6 us
    all_gather x1, blocking collectives, local(): token_grads = lax.all_gather(gradients, 'up', axis=0, tiled=True)  16.5 us
    all_gather x1, blocking collectives, local(): token_deltas = lax.all_gather(deltas, 'down', axis=0, tiled=True)  10 us
    reshape x1, local copies, waits for them, and re-layouts, local(): dec_whole = jnp.concatenate(lax.all_gather(decoder, 'down'), axis=1)  6.64 us
    dot_general x1, matrix products, local(): jnp.dot(dec_whole, lax.all_gather(enc_used, 'up', axis=0, tiled=True), pr...  6.07 us
    scatter x2, local copies, waits for them, and re-layouts, local(): jnp.zeros((UF_DEV, col_blocks, BLOCK), jnp.float32).at[:, down_blocks, :]  3.82 us
  transfers between devices with their start and end apart: 2, of which 2 were waited for; matrix products, arithmetic and copies ran while one was open for 8% of the time, Pallas kernels for 0%

profile of v1, /device:TPU:0, one launch (start us, length us, event | category | flops | bytes accessed | tf_op | source)
XLA Modules:
  0.0 144.0 jit_solution(8469344675532432315)
XLA Ops:
  6.5 0.0 copy-start
  6.5 0.0 copy-start.4
  6.5 0.0 all-gather.6.cloned.1.call-start
  6.5 0.7 all-gather.6.cloned.1.call-update
  7.3 0.0 all-gather.4.cloned.1.call-start
  7.3 0.7 compare_select_fusion
  8.0 0.0 copy-done
  8.0 0.0 copy-start.3
  8.0 0.0 copy-start.1
  8.0 0.2 copy_bitcast_fusion
  8.2 0.7 gather_fusion.1
  8.9 0.0 copy-done.4
  8.9 0.1 broadcast_bitcast_fusion
  9.0 0.9 bitcast_select_fusion
  9.9 0.0 copy-start.2
  9.9 0.0 all-gather.4.cloned.1.call-update
  9.9 0.0 copy-done.3
  10.0 0.1 copy.33
  10.1 0.0 copy-done.1
  10.1 16.5 %all_gather.16 = bf16[256,1024]{1,0:T(8,128)(2,1)S(1)} all-gather(bf16[32,1024]{1,0:T(8,128)(2,1)S(1)} %copy-done.1), channel_id=1, replica_groups=mesh['up'=8,'down'=4] {'up'}, dimensions={0}, use_global_device_ids=true | all-gather | bytes 589824 | tf_op jit(solution)/shard_map/all_gather | solution.py:15
  26.6 0.2 copy.34
  26.8 0.3 copy.35
  27.0 0.6 gather_fusion
  27.6 0.1 copy.36
  27.8 0.0 copy-done.2
  27.8 10.0 %all_gather.15 = bf16[256,512]{1,0:T(8,128)(2,1)S(1)} all-gather(bf16[64,512]{1,0:T(8,128)(2,1)S(1)} %copy-done.2), channel_id=1, replica_groups=mesh['up'=8,'down'=4] {'down'}, dimensions={0}, use_global_device_ids=true | all-gather | bytes 327680 | tf_op jit(solution)/shard_map/all_gather | solution.py:14
  37.8 0.1 bitcast_select_fusion.1
  38.0 0.1 mul.14
  38.1 0.3 fusion.1
  38.4 31.6 %all-gather.6.cloned.1.call-done = bf16[2048,1152]{1,0:T(8,128)(2,1)} async-done(((bf16[512,1152]{1,0:T(8,128)(2,1)}), bf16[2048,1152]{1,0:T(8,128)(2,1)}) %all-gather.6.cloned.1.call-update) | async-done | bytes 4718608 | tf_op jit(solution)/shard_map/all_gather | solution.py:26
  70.1 6.6 %copy.39 = bf16[512,4,1152]{0,2,1:T(8,128)(2,1)} copy(bf16[512,4,1152]{2,0,1:T(8,128)(2,1)} %bitcast.39) | data formatting | bytes 9437184 | tf_op jit(solution)/shard_map/reshape | solution.py:26
  76.7 46.2 %all-gather.4.cloned.1.call-done = bf16[4608,512]{1,0:T(8,128)(2,1)} async-done(((bf16[576,512]{1,0:T(8,128)(2,1)}), bf16[4608,512]{1,0:T(8,128)(2,1)}) %all-gather.4.cloned.1.call-update) | async-done | bytes 4718608 | tf_op jit(solution)/shard_map/all_gather | solution.py:33
  122.9 6.1 %fusion = f32[512,512]{0,1:T(8,128)S(1)} fusion(f32[512,512]{0,1:T(8,128)S(1)} %fusion.1, bf16[4608,512]{1,0:T(8,128)(2,1)} %all-gather.4.cloned.1.call-done, bf16[512,4608]{0,1:T(8,128)(2,1)} %bitcast.37), kind=kOutput, calls=%fused_computation.4 | convolution fusion | flops 2416181248 | bytes 11534336 | tf_op jit(solution)/shard_map/dot_general | solution.py:31
  129.0 1.3 copy.40
  130.3 0.1 broadcast_in_dim.33
  130.5 1.9 %scatter_fusion = f32[512,8,128]{2,0,1:T(8,128)S(1)} fusion(f32[512,8,128]{2,0,1:T(8,128)S(1)} %broadcast_in_dim.33, s32[4]{0:T(128)S(1)} %compare_select_fusion, f32[4,512,128]{2,1,0:T(8,128)} %bitcast.41), kind=kCustom, calls=%fused_computation.2 | custom fusion | bytes 3145744 | tf_op jit(solution)/shard_map/scatter | solution.py:43
  132.4 1.9 %copy.41 = f32[512,8,128]{0,2,1:T(8,128)} copy(f32[512,8,128]{2,0,1:T(8,128)S(1)} %scatter_fusion) | data formatting | bytes 4194304 | tf_op jit(solution)/shard_map/scatter | solution.py:43
  134.3 2.9 %copy.42 = f32[512,1024]{1,0:T(8,128)} copy(f32[512,1024]{0,1:T(8,128)} %bitcast.38) | data formatting | bytes 4194304 | tf_op jit(solution)/shard_map/reshape | solution.py:44
  (4 shorter events, 0.0 us)
Async XLA Ops:
  6.5 1.4 %copy-start = (bf16[576,1024]{1,0:T(8,128)(2,1)S(1)}, bf16[576,1024]{1,0:T(8,128)(2,1)}, u32[]{:S(2)}) copy-start(bf16[576,1024]{1,0:T(8,128)(2,1)} %param.11) | copy-start | bytes 3538948
  6.5 2.4 %copy-start.4 = (s32[4]{0:T(128)S(1)}, s32[4]{0:T(128)}, u32[]{:S(2)}) copy-start(s32[4]{0:T(128)} %param.9) | copy-start | bytes 52
  6.5 63.5 %all-gather.6.cloned.1.call-start = ((), (), s32[]{:S(2)}) async-start(), calls=%async_computation.1 | async-start | bytes 5898240 | tf_op jit(solution)/shard_map/all_gather | solution.py:26
  7.3 115.7 %all-gather.4.cloned.1.call-start = ((), (), s32[]{:S(2)}) async-start(), calls=%async_computation | async-start | bytes 5308416 | tf_op jit(solution)/shard_map/all_gather | solution.py:33
  8.0 2.0 %copy-start.3 = (s32[8,2]{0,1:T(2,128)S(1)}, s32[8,2]{0,1:T(2,128)}, u32[]{:S(2)}) copy-start(s32[8,2]{0,1:T(2,128)} %param.8) | copy-start | bytes 196
  8.0 2.1 %copy-start.1 = (bf16[32,1024]{1,0:T(8,128)(2,1)S(1)}, bf16[32,1024]{1,0:T(8,128)(2,1)}, u32[]{:S(2)}) copy-start(bf16[32,1024]{1,0:T(8,128)(2,1)} %param.7) | copy-start | bytes 196612
  9.9 17.9 %copy-start.2 = (bf16[64,512]{1,0:T(8,128)(2,1)S(1)}, bf16[64,512]{1,0:T(8,128)(2,1)}, u32[]{:S(2)}) copy-start(bf16[64,512]{1,0:T(8,128)(2,1)} %param.6) | copy-start | bytes 196612
Sparse Core Ops, SparseCore 0:
  9.2 60.8 all-gather.5
  71.7 51.1 all-gather.3
